TPU v7x, 32 devices: a whole 2x2x4 slice. The times are simulated.
32 devices in a mesh: gx: 2 (over core), gyz: 16 (over z, y, x).
Axes of the slice: x: 2, y: 2, z: 4, core: 2. Of those that a mesh axis runs over, the one named last changes fastest.
Arguments:
- bands: bfloat16 [16, 80, 40, 512], P('gx', 'gyz'), may hold values from -6 to 6
- potential: float32 [16, 80, 40], P('gx', 'gyz'), may hold values from 0.5 to 4
- eigenvectors: bfloat16 [512, 512], P('gyz'), may hold values from -0.25 to 0.25
Outputs:
- correlation: float32 [512, 512], P('gyz')
- hamiltonian: float32 [512, 512], P('gyz')
- rotated: bfloat16 [16, 80, 40, 512], P('gx', 'gyz')
All inputs are finite; a program needn't handle non-finite values.
Results may differ from a plain program's by a relative error of at most 0.0012.
Values may be sent and summed in bfloat16 or wider, within the bound.
A program may use at most 64 MiB of HBM per device.

v0:
```python
import jax
import jax.numpy as jnp
from jax import lax
from jax.sharding import PartitionSpec as P


def extended(block, sides, width):
    for axis, dim in sides:
        count = lax.axis_size(axis)
        forward = [(i, i + 1) for i in range(count - 1)]
        backward = [(target, source) for source, target in forward]
        low = lax.ppermute(
            lax.slice_in_dim(block, block.shape[dim] - width, None, axis=dim), axis, forward
        )
        high = lax.ppermute(lax.slice_in_dim(block, 0, width, axis=dim), axis, backward)
        block = jnp.concatenate([low, block, high], axis=dim)
    return block


def stencil(padded, potential):
    centre = padded[1:-1, 1:-1, 1:-1].astype(jnp.float32)
    neighbours = padded[2:, 1:-1, 1:-1].astype(jnp.float32) + padded[:-2, 1:-1, 1:-1].astype(
        jnp.float32
    )
    neighbours = (
        neighbours
        + padded[1:-1, 2:, 1:-1].astype(jnp.float32)
        + padded[1:-1, :-2, 1:-1].astype(jnp.float32)
    )
    neighbours = (
        neighbours
        + padded[1:-1, 1:-1, 2:].astype(jnp.float32)
        + padded[1:-1, 1:-1, :-2].astype(jnp.float32)
    )
    return ((3.0 + potential[..., None]) * centre - 0.5 * neighbours).astype(jnp.bfloat16)


def on_device(bands, potential, eigenvectors):
    halo_bands = extended(bands, (("gx", 0), ("gyz", 1)), 1)
    padded = jnp.pad(halo_bands, ((0, 0), (0, 0), (1, 1), (0, 0)))
    hamil_bands = stencil(padded, potential)
    band_count = bands.shape[3]
    cell_count = bands.shape[0] * bands.shape[1] * bands.shape[2]
    flat_bands = bands.reshape(cell_count, band_count)
    combined = jnp.concatenate((flat_bands, hamil_bands.reshape(cell_count, band_count)), axis=1)
    inv_volume = 1.0 / (cell_count * lax.axis_size("gyz"))
    product = lax.dot_general(
        flat_bands, combined, (((0,), (0,)), ((), ())), preferred_element_type=jnp.float32
    )
    row_terms = lax.psum_scatter(product * inv_volume, "gyz", scatter_dimension=0, tiled=True)
    gram_block = lax.psum(row_terms, "gx")
    coefficients = lax.all_gather(eigenvectors, "gyz", axis=0, tiled=True)
    rotated = jnp.dot(flat_bands, coefficients, preferred_element_type=jnp.float32)
    return (
        gram_block[:, :band_count],
        gram_block[:, band_count:],
        rotated.astype(jnp.bfloat16).reshape(bands.shape),
    )


def solution(mesh):
    in_specs = (P("gx", "gyz", None, None), P("gx", "gyz", None), P("gyz", None))
    out_specs = (P("gyz", None), P("gyz", None), P("gx", "gyz", None, None))
    return jax.shard_map(
        on_device, mesh=mesh, in_specs=in_specs, out_specs=out_specs, check_vma=False
    )
```

profile of v0, /device:TPU:0, one launch (start us, length us, event | category | flops | bytes accessed | tf_op | source)
XLA Modules:
  0.0 162.3 jit_solution(2966103501217675455)
XLA Ops:
  7.2 0.0 reduce-scatter.4.cloned.1.call-start
  7.2 1.1 fusion.14
  8.3 2.4 %collective-permute-start.1 = (bf16[1,5,40,512]{3,2,1,0:T(8,128)(2,1)S(1)}, bf16[1,5,40,512]{3,2,1,0:T(8,128)(2,1)S(1)}, u32[]{:S(2)}, u32[]{:S(2)}) collective-permute-start(bf16[1,5,40,512]{3,2,1,0:T(8,128)(2,1)S(1)} %get-tuple-element.12), channel_id=1, source_target_pairs={{0,16},{1,17},{2,18},{3,19},{4,20},{5,21},{6,22},{7,23},{8,24},{9,... | collective-permute-start | bytes 614408 | tf_op jit(solution)/shard_map/ppermute | solution.py:12
  10.7 1.3 collective-permute-start
  12.0 0.0 collective-permute-done.1
  12.0 0.0 copy-start.2
  12.0 1.5 constant_dynamic-update-slice_fusion.1
  13.6 0.5 collective-permute-done
  14.1 0.1 fusion.13
  14.1 1.3 collective-permute-start.2
  15.4 4.9 %collective-permute-start.3 = (bf16[10,1,40,512]{3,2,1,0:T(8,128)(2,1)S(1)}, bf16[10,1,40,512]{3,2,1,0:T(8,128)(2,1)S(1)}, u32[]{:S(2)}, u32[]{:S(2)}) collective-permute-start(bf16[10,1,40,512]{3,2,1,0:T(8,128)(2,1)S(1)} %get-tuple-element.9), channel_id=1, source_target_pairs={{0,1},{1,2},{2,3},{3,4},{4,5},{5,6},{6,7},{7,8},{8,9},{9,10},{10,1... | collective-permute-start | bytes 1228808 | tf_op jit(solution)/shard_map/ppermute | solution.py:12
  20.3 0.0 copy-done.2
  20.3 0.0 copy-start
  20.3 8.3 %collective-permute-done.2 = bf16[10,1,40,512]{3,2,1,0:T(8,128)(2,1)S(1)} collective-permute-done((bf16[10,1,40,512]{3,2,1,0:T(8,128)(2,1)S(1)}, bf16[10,1,40,512]{3,2,1,0:T(8,128)(2,1)S(1)}, u32[]{:S(2)}, u32[]{:S(2)}) %collective-permute-start.2) | collective-permute-done | bytes 409632 | tf_op jit(solution)/shard_map/ppermute | solution.py:15
  28.6 9.9 %collective-permute-done.3 = bf16[10,1,40,512]{3,2,1,0:T(8,128)(2,1)S(1)} collective-permute-done((bf16[10,1,40,512]{3,2,1,0:T(8,128)(2,1)S(1)}, bf16[10,1,40,512]{3,2,1,0:T(8,128)(2,1)S(1)}, u32[]{:S(2)}, u32[]{:S(2)}) %collective-permute-start.3) | collective-permute-done | bytes 409632 | tf_op jit(solution)/shard_map/ppermute | solution.py:12
  38.6 1.7 %fusion.5 = bf16[10,7,42,512]{3,2,1,0:T(8,128)(2,1)S(1)} fusion(bf16[10,1,40,512]{3,2,1,0:T(8,128)(2,1)S(1)} %collective-permute-done.2, bf16[10,5,40,512]{3,2,1,0:T(8,128)(2,1)S(1)} %constant_dynamic-update-slice_fusion, bf16[10,1,40,512]{3,2,1,0:T(8,128)(2,1)S(1)} %collective-permute-done.3), kind=kLoop, calls=%fused_computation.7 | loop fusion | flops 18063360 | bytes 5877760 | tf_op jit(solution)/shard_map/concatenate | solution.py:16
  40.3 0.0 copy-done
  40.3 3.3 %subtract_convert_fusion = bf16[8,5,40,512]{3,2,1,0:T(8,128)(2,1)S(1)} fusion(bf16[8,5,40,512]{3,2,1,0:T(8,128)(2,1)S(1)} %copy-done, bf16[10,7,42,512]{3,2,1,0:T(8,128)(2,1)S(1)} %fusion.5, bf16[10,5,40,512]{3,2,1,0:T(8,128)(2,1)S(1)} %constant_dynamic-update-slice_fusion, bf16[10,1,40,512]{3,2,1,0:T(8,128)(2,1)S(1)} %collective-permute-done.3, ...), kind=kLoop, calls=%fused_computation.12 | loop fusion | flops 16384000 | bytes 9836800 | tf_op jit(solution)/shard_map/convert_element_type | solution.py:35
  43.6 3.4 %multiply_bitcast_fusion = f32[512,1024]{0,1:T(8,128)} fusion(bf16[1600,512]{1,0:T(8,128)(2,1)S(1)} %bitcast.9, bf16[1600,512]{1,0:T(8,128)(2,1)S(1)} %bitcast.11), kind=kOutput, calls=%fused_computation.14 | convolution fusion | flops 1684799488 | bytes 5373952 | tf_op jit(solution)/shard_map/dot_general | solution.py:47
  47.0 2.9 %copy.12 = f32[512,1024]{1,0:T(8,128)} copy(f32[512,1024]{0,1:T(8,128)} %multiply_bitcast_fusion) | data formatting | bytes 4194304
  50.0 0.0 copy-start.1
  50.0 0.0 reduce-scatter.4.cloned.1.call-update
  50.0 0.0 all-reduce.3.cloned.1.call-start
  50.0 0.7 copy-done.1
  50.7 46.1 %all_gather.3 = bf16[512,512]{1,0:T(8,128)(2,1)S(1)} all-gather(bf16[32,512]{1,0:T(8,128)(2,1)S(1)} %copy-done.1), channel_id=1, replica_groups=mesh['gx'=2,'gyz'=16] {'gyz'}, dimensions={0}, use_global_device_ids=true | all-gather | bytes 557056 | tf_op jit(solution)/shard_map/all_gather | solution.py:52
  96.9 36.3 %reduce-scatter.4.cloned.1.call-done = f32[32,1024]{1,0:T(8,128)} async-done(((f32[512,1024]{1,0:T(8,128)}), f32[32,1024]{1,0:T(8,128)}) %reduce-scatter.4.cloned.1.call-update) | async-done | bytes 131088
  133.1 1.9 %copy.13 = f32[32,1024]{0,1:T(8,128)} copy(f32[32,1024]{1,0:T(8,128)} %reduce-scatter.4.cloned.1.call-done) | data formatting | bytes 262144
  135.1 0.0 all-reduce.3.cloned.1.call-update
  135.1 2.2 %convolution_convert_fusion = bf16[1600,512]{1,0:T(8,128)(2,1)} fusion(bf16[1600,512]{1,0:T(8,128)(2,1)S(1)} %bitcast.10, bf16[512,512]{1,0:T(8,128)(2,1)S(1)} %all_gather.3), kind=kOutput, calls=%fused_computation.13 | convolution fusion | flops 839680000 | bytes 3801088 | tf_op jit(solution)/shard_map/dot_general | solution.py:53
  137.3 15.7 %all-reduce.3.cloned.1.call-done = f32[32,1024]{0,1:T(8,128)} async-done(((f32[32,1024]{0,1:T(8,128)}), f32[32,1024]{0,1:T(8,128)}) %all-reduce.3.cloned.1.call-update) | async-done | bytes 131088 | tf_op jit(solution)/shard_map/psum | solution.py:51
  152.9 1.1 fusion.15
  154.0 0.7 copy.10
  154.7 0.7 copy.11
  (4 shorter events, 0.0 us)
Async XLA Ops:
  7.2 126.0 %reduce-scatter.4.cloned.1.call-start = ((), (), s32[]{:S(2)}) async-start(), calls=%async_computation.2 | async-start | bytes 2228224
  8.3 3.7 %collective-permute-start.1 = (bf16[1,5,40,512]{3,2,1,0:T(8,128)(2,1)S(1)}, bf16[1,5,40,512]{3,2,1,0:T(8,128)(2,1)S(1)}, u32[]{:S(2)}, u32[]{:S(2)}) collective-permute-start(bf16[1,5,40,512]{3,2,1,0:T(8,128)(2,1)S(1)} %get-tuple-element.12), channel_id=1, source_target_pairs={{0,16},{1,17},{2,18},{3,19},{4,20},{5,21},{6,22},{7,23},{8,24},{9,... | collective-permute-start | bytes 614408 | tf_op jit(solution)/shard_map/ppermute | solution.py:12
  10.7 3.3 %collective-permute-start = (bf16[1,5,40,512]{3,2,1,0:T(8,128)(2,1)S(1)}, bf16[1,5,40,512]{3,2,1,0:T(8,128)(2,1)S(1)}, u32[]{:S(2)}, u32[]{:S(2)}) collective-permute-start(bf16[1,5,40,512]{3,2,1,0:T(8,128)(2,1)S(1)} %get-tuple-element.11), channel_id=1, source_target_pairs={{16,0},{17,1},{18,2},{19,3},{20,4},{21,5},{22,6},{23,7},{24,8},{25... | collective-permute-start | bytes 614408 | tf_op jit(solution)/shard_map/ppermute | solution.py:15
  12.0 8.3 %copy-start.2 = (f32[8,5,40]{2,0,1:T(8,128)S(1)}, f32[8,5,40]{2,0,1:T(8,128)}, u32[]{:S(2)}) copy-start(f32[8,5,40]{2,0,1:T(8,128)} %param.4) | copy-start | bytes 19204
  14.1 14.5 %collective-permute-start.2 = (bf16[10,1,40,512]{3,2,1,0:T(8,128)(2,1)S(1)}, bf16[10,1,40,512]{3,2,1,0:T(8,128)(2,1)S(1)}, u32[]{:S(2)}, u32[]{:S(2)}) collective-permute-start(bf16[10,1,40,512]{3,2,1,0:T(8,128)(2,1)S(1)} %get-tuple-element.10), channel_id=1, source_target_pairs={{1,0},{2,1},{3,2},{4,3},{5,4},{6,5},{7,6},{8,7},{9,8},{10,9},{11,1... | collective-permute-start | bytes 1228808 | tf_op jit(solution)/shard_map/ppermute | solution.py:15
  15.4 23.1 %collective-permute-start.3 = (bf16[10,1,40,512]{3,2,1,0:T(8,128)(2,1)S(1)}, bf16[10,1,40,512]{3,2,1,0:T(8,128)(2,1)S(1)}, u32[]{:S(2)}, u32[]{:S(2)}) collective-permute-start(bf16[10,1,40,512]{3,2,1,0:T(8,128)(2,1)S(1)} %get-tuple-element.9), channel_id=1, source_target_pairs={{0,1},{1,2},{2,3},{3,4},{4,5},{5,6},{6,7},{7,8},{8,9},{9,10},{10,1... | collective-permute-start | bytes 1228808 | tf_op jit(solution)/shard_map/ppermute | solution.py:12
  20.3 19.9 %copy-start = (bf16[8,5,40,512]{3,2,1,0:T(8,128)(2,1)S(1)}, bf16[8,5,40,512]{3,2,1,0:T(8,128)(2,1)}, u32[]{:S(2)}) copy-start(bf16[8,5,40,512]{3,2,1,0:T(8,128)(2,1)} %param.3) | copy-start | bytes 4915204
  50.0 0.8 copy-start.1
  50.0 102.9 %all-reduce.3.cloned.1.call-start = ((), (), s32[]{:S(2)}) async-start(), calls=%async_computation.1 | async-start | bytes 1048576 | tf_op jit(solution)/shard_map/psum | solution.py:51
Sparse Core Ops, SparseCore 0:
  50.1 82.9 reduce-scatter.3
  135.5 17.3 all-reduce.2
where the time goes:
time: 163 us; the launch traced here: 162 us
  waiting for transfers between devices  70.7 us (43%)
  blocking collectives  46.1 us (28%)
  between operations  14.2 us (9%)
  local copies, waits for them, and re-layouts  10.8 us (7%)
  starting transfers between devices  9.94 us (6%)
  matrix products  5.59 us (3%)
  other arithmetic  5.03 us (3%)
    all_gather x1, blocking collectives, on_device(): coefficients = lax.all_gather(eigenvectors, 'gyz', axis=0, tiled=True)  46.1 us
    unnamed x3, waiting for transfers between devices  36.3 us
    psum x1, waiting for transfers between devices, on_device(): gram_block = lax.psum(row_terms, 'gx')  15.7 us
    ppermute x2, waiting for transfers between devices, extended(): lax.ppermute(lax.slice_in_dim(block, block.shape[dim] - width, None, axis...  9.91 us
    ppermute x2, waiting for transfers between devices, extended(): lax.ppermute(lax.slice_in_dim(block, 0, width, axis=dim), axis, backward)  8.75 us
    unnamed x12, local copies, waits for them, and re-layouts  8.56 us
    ppermute x2, starting transfers between devices, extended(): lax.ppermute(lax.slice_in_dim(block, block.shape[dim] - width, None, axis...  7.28 us
    dot_general x1, matrix products, on_device(): lax.dot_general(flat_bands, combined, (((0,), (0,)), ((), ())), preferred...  3.41 us
  transfers between devices with their start and end apart: 6, of which 5 were waited for; matrix products, arithmetic and copies ran while one was open for 2% of the time, Pallas kernels for 0%

commit v1 on v0

v1 whole, which is shorter than its diff:
```python
import functools
import itertools

import jax
import jax.numpy as jnp
from jax import lax
from jax.experimental import pallas as pl
from jax.experimental.pallas import tpu as pltpu
from jax.sharding import PartitionSpec as P

MESH = pl.DeviceIdType.MESH
F32 = jnp.float32


def digit_sizes(count):
    sizes = []
    while count > 1:
        size = 4 if count % 4 == 0 else (2 if count % 2 == 0 else count)
        sizes.append(size)
        count //= size
    return tuple(reversed(sizes)) or (1,)


def gram_t(left, right):
    return lax.dot_general(left, right, (((0,), (0,)), ((), ())), preferred_element_type=F32)


class Copies:
    def __init__(self, send_sems, recv_sems):
        self.send_sems, self.recv_sems, self.used = send_sems, recv_sems, 0

    def make(self, src, dst, device_id):
        slot = self.used
        self.used += 1
        return pltpu.make_async_remote_copy(
            src_ref=src, dst_ref=dst, send_sem=self.send_sems.at[slot],
            recv_sem=self.recv_sems.at[slot], device_id=device_id, device_id_type=MESH)


def kernel(geometry, grid4, flat, pot, eig, corr_out, ham_out, coef, padded, hq, corr, ham,
           halo_y, halo_x, pair_c, pair_h, sum_c, sum_h, *rest):
    gx_size, gyz_size, cx, cy, cz, bands, rows, sizes, copy_count = geometry
    count = len(sizes)
    recv_c, part_c = rest[:count], rest[count:2 * count]
    recv_h, part_h = rest[2 * count:3 * count], rest[3 * count:4 * count]
    gx_c, gx_h, final_c, final_h, send_sems, recv_sems = rest[4 * count:]
    half = bands // 2
    gx, gyz = lax.axis_index("gx"), lax.axis_index("gyz")
    parity = lax.rem(gx, 2)
    partner = gx + 1 - 2 * parity
    mine = pl.ds(pl.multiple_of(parity * half, half), half)
    other = pl.ds(pl.multiple_of((1 - parity) * half, half), half)
    strides = []
    step = gyz_size
    for size in sizes:
        step //= size
        strides.append(step)
    digits = [lax.rem(gyz // stride, size) for stride, size in zip(strides, sizes)]
    copies = Copies(send_sems, recv_sems)

    def peer(d, k):
        digit = lax.rem(digits[d] + k, sizes[d])
        return gyz + (digit - digits[d]) * strides[d], digit

    coef[tuple(digits) + (slice(None), mine)] = eig[:, mine]

    barrier = pltpu.get_barrier_semaphore()
    greeted = [(gx, lax.rem(gyz + 1, gyz_size)), (gx, lax.rem(gyz + gyz_size - 1, gyz_size)),
               (lax.rem(gx + 1, gx_size), gyz), (lax.rem(gx + gx_size - 1, gx_size), gyz),
               (partner, gyz)]
    for d, size in enumerate(sizes):
        greeted += [(gx, peer(d, k)[0]) for k in range(1, size)]
    greeted += [(lax.rem(gx + 2 * k, gx_size), gyz) for k in range(1, gx_size // 2)]
    for device in greeted:
        pl.semaphore_signal(barrier, inc=1, device_id=device, device_id_type=MESH)
    pl.semaphore_wait(barrier, len(greeted))

    to_x = copies.make(grid4.at[cx - 1], halo_x, (lax.rem(gx + 1, gx_size), gyz))
    to_y = copies.make(grid4.at[:, cy - 1], halo_y, (gx, lax.rem(gyz + 1, gyz_size)))
    last_x, last_y = gx == gx_size - 1, gyz == gyz_size - 1

    @pl.when(jnp.logical_not(last_y))
    def _():
        to_y.start()

    @pl.when(jnp.logical_not(last_x))
    def _():
        to_x.start()

    @pl.when(gx == 0)
    def _():
        halo_x[...] = jnp.zeros_like(halo_x)

    @pl.when(gyz == 0)
    def _():
        halo_y[...] = jnp.zeros_like(halo_y)

    def coef_phase(d):
        started = []
        for k in range(1, sizes[d]):
            index = tuple([slice(None)] * d + digits[d:]) + (slice(None), mine)
            block = coef.at[index]
            copy = copies.make(block, block, (gx, peer(d, k)[0]))
            copy.start()
            started.append(copy)
        return started

    def exchange(d, source, received, done):
        started = []
        left = [i for i in range(count) if i not in done]
        for k in range(1, sizes[d]):
            target, digit = peer(d, k)
            index = tuple(digit if i == d else slice(None) for i in left)
            copy = copies.make(source.at[index], received.at[k - 1], (gx, target))
            copy.start()
            started.append(copy)
        return started

    def reduced(d, source, received, result, done, started):
        left = [i for i in range(count) if i not in done]
        index = tuple(digits[d] if i == d else slice(None) for i in left)
        for copy in started:
            copy.wait_recv()
        total = source[index]
        for k in range(1, sizes[d]):
            total = total + received[k - 1]
        result[...] = total
        sent.extend(started)

    sent = []

    def store_rows(target, first, value):
        for j in range(value.shape[0] // rows):
            index, rest_of = [], first // rows + j
            for stride in strides:
                index.append(rest_of // stride)
                rest_of %= stride
            target[tuple(index)] = value[j * rows:(j + 1) * rows]

    tile = min(bands, 256)
    coef_copies = coef_phase(0)
    for first in range(0, bands, tile):
        store_rows(corr, first, gram_t(flat[:, first:first + tile], flat[...]))
    everything = tuple([slice(None)] * (count + 1))
    pair_copy_c = copies.make(corr.at[everything + (other,)], pair_c, (partner, gyz))
    pair_copy_c.start()

    plane = cy * cz
    cells = cx * plane
    chunk = 2 * cz if cells % (2 * cz) == 0 else cz
    for first in range(0, cells, chunk):
        padded[first:first + chunk] = flat[first:first + chunk].astype(F32)
    row = lax.broadcasted_iota(jnp.int32, (cz, cz), 0)
    column = lax.broadcasted_iota(jnp.int32, (cz, cz), 1)
    zero_row = jnp.zeros((1, bands), F32)

    def segment(x, y):
        at = x * plane + y * cz
        centre = padded[at:at + cz]
        near = jnp.concatenate([zero_row, centre[:-1]]) + jnp.concatenate([centre[1:], zero_row])
        for there, offset in ((x > 0, -plane), (x < cx - 1, plane), (y > 0, -cz), (y < cy - 1, cz)):
            if there:
                near = near + padded[at + offset:at + offset + cz]
        local = jnp.broadcast_to(pot[x, y:y + 1, :], (cz, cz))
        factor = 3.0 + jnp.sum(jnp.where(row == column, local, 0.0), axis=1, keepdims=True)
        return factor * centre - 0.5 * near

    order = list(itertools.product(range(cx), range(cy)))
    per = chunk // cz
    for first in range(0, len(order), per):
        hq[first * cz:(first + per) * cz] = jnp.concatenate(
            [segment(*xy) for xy in order[first:first + per]]).astype(jnp.bfloat16)

    pair_copy_c.wait_recv()
    sum_c[...] = corr[everything + (mine,)] + pair_c[...]
    c_started = exchange(0, sum_c, recv_c[0], ())
    if count > 1:
        for copy in coef_copies:
            copy.wait_recv()
        sent.extend(coef_copies)
        coef_copies = coef_phase(1)

    for first in range(0, bands, tile):
        store_rows(ham, first, gram_t(flat[:, first:first + tile], hq[...]))

    @pl.when(gyz > 0)
    def _():
        to_y.wait_recv()

    @pl.when(gx > 0)
    def _():
        to_x.wait_recv()

    first_y = jnp.concatenate([flat[x * plane:x * plane + cz] for x in range(cx)])
    ghost_y = jnp.concatenate([halo_y[x] for x in range(cx)])
    first_x = flat[0:plane]
    ghost_x = jnp.concatenate([halo_x[y] for y in range(cy)])
    cross = padded.at[0:bands]
    for first in range(0, bands, tile):
        cut = slice(first, first + tile)
        cross[cut] = -0.5 * (gram_t(first_y[:, cut], ghost_y) + gram_t(first_x[:, cut], ghost_x))
    for first in range(0, bands, tile):
        cut = slice(first, first + tile)
        value = cross[cut] + jnp.transpose(cross[:, cut])
        for j in range(tile // rows):
            index, rest_of = [], first // rows + j
            for stride in strides:
                index.append(rest_of // stride)
                rest_of %= stride
            index = tuple(index)
            ham[index] = ham[index] + value[j * rows:(j + 1) * rows]
    pair_copy_h = copies.make(ham.at[everything + (other,)], pair_h, (partner, gyz))
    pair_copy_h.start()

    reduced(0, sum_c, recv_c[0], part_c[0], (), c_started)
    done_c, source_c = [0], part_c[0]
    if count > 1:
        c_started = exchange(1, source_c, recv_c[1], done_c)

    pair_copy_h.wait_recv()
    sum_h[...] = ham[everything + (mine,)] + pair_h[...]
    order_h = list(range(count))[::-1]
    h_started = exchange(order_h[0], sum_h, recv_h[0], ())

    for d in range(1, count):
        for copy in coef_copies:
            copy.wait_recv()
        sent.extend(coef_copies)
        coef_copies = coef_phase(d + 1) if d + 1 < count else []
    for copy in coef_copies:
        copy.wait_recv()
    sent.extend(coef_copies)
    mine_block = coef.at[everything + (mine,)]
    pair_copy_e = copies.make(mine_block, mine_block, (partner, gyz))
    pair_copy_e.start()

    scale = 1.0 / (cells * gyz_size)

    def finish(source, gx_recv, final, out):
        others = []
        for k in range(1, gx_size // 2):
            copy = copies.make(source, gx_recv.at[k - 1], (lax.rem(gx + 2 * k, gx_size), gyz))
            copy.start()
            others.append(copy)
        for copy in others:
            copy.wait_recv()
        sent.extend(others)
        total = source[...]
        for k in range(1, gx_size // 2):
            total = total + gx_recv[k - 1]
        final[:, mine] = total * scale
        copy = copies.make(final.at[:, mine], final.at[:, mine], (partner, gyz))
        copy.start()
        return copy

    for d in range(1, count):
        reduced(d, source_c, recv_c[d], part_c[d], done_c, c_started)
        done_c, source_c = done_c + [d], part_c[d]
        if d + 1 < count:
            c_started = exchange(d + 1, source_c, recv_c[d + 1], done_c)
    last_c = finish(source_c, gx_c, final_c, corr_out)

    done_h, source_h = [], sum_h
    for i, d in enumerate(order_h):
        reduced(d, source_h, recv_h[i], part_h[i], done_h, h_started)
        done_h, source_h = done_h + [d], part_h[i]
        if i + 1 < count:
            h_started = exchange(order_h[i + 1], source_h, recv_h[i + 1], done_h)
    last_h = finish(source_h, gx_h, final_h, ham_out)

    last_c.wait_recv()
    corr_out[...] = final_c[...]
    pair_copy_e.wait_recv()
    last_h.wait_recv()
    ham_out[...] = final_h[...]
    for copy in sent + [pair_copy_c, pair_copy_h, pair_copy_e, last_c, last_h]:
        copy.wait_send()

    @pl.when(jnp.logical_not(last_y))
    def _():
        to_y.wait_send()

    @pl.when(jnp.logical_not(last_x))
    def _():
        to_x.wait_send()

    assert copies.used == copy_count


def on_device(bands, potential, eigenvectors):
    gx_size, gyz_size = lax.axis_size("gx"), lax.axis_size("gyz")
    cx, cy, cz, width = bands.shape
    rows = eigenvectors.shape[0]
    cells = cx * cy * cz
    sizes = digit_sizes(gyz_size)
    count = len(sizes)
    half = width // 2
    flat = bands.reshape(cells, width)
    copy_count = 2 + 3 * sum(s - 1 for s in sizes) + 3 + 2 * (gx_size // 2)
    geometry = (gx_size, gyz_size, cx, cy, cz, width, rows, sizes, copy_count)

    def stages(order):
        received, parts, left = [], [], list(range(count))
        for d in order:
            left.remove(d)
            shape = tuple(sizes[i] for i in left) + (rows, half)
            received.append(pltpu.VMEM((sizes[d] - 1,) + shape, F32))
            parts.append(pltpu.VMEM(shape, F32))
        return received + parts

    wide, narrow = sizes + (rows, width), sizes + (rows, half)
    others = max(gx_size // 2 - 1, 1)
    vmem = pl.BlockSpec(memory_space=pltpu.VMEM)
    corr, ham, coef = pl.pallas_call(
        functools.partial(kernel, geometry),
        out_shape=(jax.ShapeDtypeStruct((rows, width), F32), jax.ShapeDtypeStruct((rows, width), F32),
                   jax.ShapeDtypeStruct(wide, jnp.bfloat16)),
        in_specs=[pl.BlockSpec(memory_space=pl.ANY), vmem, vmem, vmem],
        out_specs=(vmem, vmem, vmem),
        scratch_shapes=[
            pltpu.VMEM((cells, width), F32), pltpu.VMEM((cells, width), jnp.bfloat16),
            pltpu.VMEM(wide, F32), pltpu.VMEM(wide, F32),
            pltpu.VMEM((cx, cz, width), jnp.bfloat16), pltpu.VMEM((cy, cz, width), jnp.bfloat16),
            pltpu.VMEM(narrow, F32), pltpu.VMEM(narrow, F32),
            pltpu.VMEM(narrow, F32), pltpu.VMEM(narrow, F32),
            *stages(range(count)), *stages(range(count - 1, -1, -1)),
            pltpu.VMEM((others, rows, half), F32), pltpu.VMEM((others, rows, half), F32),
            pltpu.VMEM((rows, width), F32), pltpu.VMEM((rows, width), F32),
            pltpu.SemaphoreType.DMA((copy_count,)), pltpu.SemaphoreType.DMA((copy_count,)),
        ],
        compiler_params=pltpu.CompilerParams(
            collective_id=0, has_side_effects=True, vmem_limit_bytes=52 * 1024 * 1024),
    )(bands, flat, potential, eigenvectors)
    rotated = jnp.dot(flat, coef.reshape(width, width), preferred_element_type=F32)
    return corr, ham, rotated.astype(jnp.bfloat16).reshape(bands.shape)


def solution(mesh):
    in_specs = (P("gx", "gyz", None, None), P("gx", "gyz", None), P("gyz", None))
    out_specs = (P("gyz", None), P("gyz", None), P("gx", "gyz", None, None))
    return jax.shard_map(
        on_device, mesh=mesh, in_specs=in_specs, out_specs=out_specs, check_vma=False
    )
```

time: 163 us -> 46.8 us (0.29)
  waiting for transfers between devices: 70.7 us -> 0 us
  blocking collectives: 46.1 us -> 0 us
  Pallas kernels: 0 us -> 41 us
  between operations: 14.2 us -> 0.65 us
  starting transfers between devices: 9.94 us -> 0 us
  local copies, waits for them, and re-layouts: 10.8 us -> 2.75 us
  other arithmetic: 5.03 us -> 0 us
  matrix products: 5.59 us -> 2.18 us
    all_gather x1 -> x0, blocking collectives: 46.1 us -> none  [on_device(): coefficients = lax.all_gather(eigenvectors, 'gyz', axis=0, tiled=True)]
    pallas_call x0 -> x1, Pallas kernels: none -> 41 us  [on_device(): pl.pallas_call(functools.partial(kernel, geometry), out_shape=(jax.ShapeD...]
    unnamed x3 -> x0, waiting for transfers between devices: 36.3 us -> none
    ppermute x4 -> x0, waiting for transfers between devices: 18.7 us -> none  [the longest x2 9.91 us: extended(): lax.ppermute(lax.slice_in_dim(block, block.shape[dim] - width, None, axis...]
    psum x1 -> x0, waiting for transfers between devices: 15.7 us -> none  [on_device(): gram_block = lax.psum(row_terms, 'gx')]
    ppermute x4 -> x0, starting transfers between devices: 9.86 us -> none  [the longest x2 7.28 us: extended(): lax.ppermute(lax.slice_in_dim(block, block.shape[dim] - width, None, axis...]
    unnamed x12 -> x7, local copies, waits for them, and re-layouts: 8.56 us -> 2.75 us
    dot_general x2 -> x1, matrix products: 5.59 us -> 2.18 us  [on_device(): jnp.dot(flat, coef.reshape(width, width), preferred_element_type=F32)]
  transfers between devices with their start and end apart: 6 -> 0, of which waited for: 5 -> 0; matrix products, arithmetic and copies ran while one was open for 2% -> 0% of each run, Pallas kernels for 0% -> 0%
where the time goes in v1:
time: 46.8 us; the launch traced here: 46.6 us
  Pallas kernels  41 us (88%)
  local copies, waits for them, and re-layouts  2.75 us (6%)
  matrix products  2.18 us (5%)
  between operations  0.65 us (1%)
    pallas_call x1, Pallas kernels, on_device(): pl.pallas_call(functools.partial(kernel, geometry), out_shape=(jax.ShapeD...  41 us
    unnamed x7, local copies, waits for them, and re-layouts  2.75 us
    dot_general x1, matrix products, on_device(): jnp.dot(flat, coef.reshape(width, width), preferred_element_type=F32)  2.18 us

profile of v1, /device:TPU:0, one launch (start us, length us, event | category | flops | bytes accessed | tf_op | source)
XLA Modules:
  0.0 46.6 jit_solution(10575270623018685245)
XLA Ops:
  0.6 0.7 %copy.6.pot = f32[8,5,40]{2,1,0:T(8,128)S(1)} copy(f32[8,5,40]{2,0,1:T(8,128)} %param.4) | data formatting | bytes 12800 | tf_op args[1]
  1.4 0.0 copy-start
  1.4 0.8 %copy-done = bf16[32,512]{1,0:T(8,128)(2,1)S(1)} copy-done((bf16[32,512]{1,0:T(8,128)(2,1)S(1)}, bf16[32,512]{1,0:T(8,128)(2,1)}, u32[]{:S(2)}) %copy-start) | copy-done | bytes 32792
  2.1 0.0 copy-start.1
  2.1 41.0 %shard_map.58 = (f32[32,512]{1,0:T(8,128)S(1)}, f32[32,512]{1,0:T(8,128)S(1)}, bf16[4,4,32,512]{3,2,1,0:T(8,128)(2,1)S(1)}) custom-call(bf16[8,5,40,512]{3,2,1,0:T(8,128)(2,1)} %grid4.1, bf16[1600,512]{1,0:T(8,128)(2,1)} %bitcast.8, f32[8,5,40]{2,1,0:T(8,128)S(1)} %copy.6.pot, bf16[32,512]{1,0:T(8,128)(2,1)S(1)} %copy-done), custom_call_target="tpu_custom_call" | custom-call | tf_op jit(solution)/shard_map/pallas_call | solution.py:314
  43.2 0.0 copy-done.1
  43.2 2.2 %convolution_convert_fusion = bf16[512,1600]{0,1:T(8,128)(2,1)} fusion(bf16[1600,512]{1,0:T(8,128)(2,1)S(1)} %bitcast.9, bf16[512,512]{1,0:T(8,128)(2,1)S(1)} %bitcast.7), kind=kOutput, calls=%fused_computation | convolution fusion | flops 839680000 | bytes 3801088 | tf_op jit(solution)/shard_map/dot_general | solution.py:334
  45.3 0.6 %copy.9 = f32[32,512]{1,0:T(8,128)} copy(f32[32,512]{1,0:T(8,128)S(1)} %get-tuple-element.12) | data formatting | bytes 131072
  46.0 0.6 %copy.10 = f32[32,512]{1,0:T(8,128)} copy(f32[32,512]{1,0:T(8,128)S(1)} %get-tuple-element.13) | data formatting | bytes 131072
Async XLA Ops:
  1.4 0.8 %copy-start = (bf16[32,512]{1,0:T(8,128)(2,1)S(1)}, bf16[32,512]{1,0:T(8,128)(2,1)}, u32[]{:S(2)}) copy-start(bf16[32,512]{1,0:T(8,128)(2,1)} %eig.1) | copy-start | bytes 98308
  2.1 41.0 %copy-start.1 = (bf16[8,5,40,512]{3,2,1,0:T(8,128)(2,1)S(1)}, bf16[8,5,40,512]{3,2,1,0:T(8,128)(2,1)}, u32[]{:S(2)}) copy-start(bf16[8,5,40,512]{3,2,1,0:T(8,128)(2,1)} %grid4.1) | copy-start | bytes 4915204

commit v2 on v1

v2 whole, which is shorter than its diff:
```python
import functools
import itertools

import jax
import jax.numpy as jnp
from jax import lax
from jax.experimental import pallas as pl
from jax.experimental.pallas import tpu as pltpu
from jax.sharding import PartitionSpec as P

MESH = pl.DeviceIdType.MESH
F32 = jnp.float32


def digit_sizes(count):
    sizes = []
    while count > 1:
        size = 4 if count % 4 == 0 else (2 if count % 2 == 0 else count)
        sizes.append(size)
        count //= size
    return tuple(reversed(sizes)) or (1,)


def gram_t(left, right):
    return lax.dot_general(left, right, (((0,), (0,)), ((), ())), preferred_element_type=F32)


class Copies:
    def __init__(self, send_sems, recv_sems):
        self.send_sems, self.recv_sems, self.used = send_sems, recv_sems, 0

    def make(self, src, dst, device_id):
        slot = self.used
        self.used += 1
        return pltpu.make_async_remote_copy(
            src_ref=src, dst_ref=dst, send_sem=self.send_sems.at[slot],
            recv_sem=self.recv_sems.at[slot], device_id=device_id, device_id_type=MESH)


def streams_of(rows, count):
    fast, slow = tuple(range(count))[::-1], tuple(range(count))
    if rows % 32 == 0 and count > 1:
        cut = rows // 4
        return ((0, cut * H_PARTS, fast), (cut * H_PARTS, rows, slow)), ((0, cut * C_PARTS, fast), (cut * C_PARTS, rows, slow))
    return ((0, rows, fast),), ((0, rows, fast),)


H_PARTS, C_PARTS = 3, 2


class Stream:
    def __init__(self, context, source, first, last, order, received, parts):
        self.context, self.source, self.order = context, source, order
        self.rows, self.received, self.parts = slice(first, last), received, parts
        self.left, self.phase = list(range(len(order))), 0

    def index(self, value):
        d = self.order[self.phase]
        at = tuple(value if i == d else slice(None) for i in self.left)
        return at + (self.rows,) if self.phase == 0 else at

    def start(self):
        copies, sizes, digits, gx, peer = self.context
        d = self.order[self.phase]
        self.flying = []
        for k in range(1, sizes[d]):
            target, digit = peer(d, k)
            copy = copies.make(self.source.at[self.index(digit)],
                               self.received[self.phase].at[k - 1], (gx, target))
            copy.start()
            self.flying.append(copy)

    def finish(self):
        copies, sizes, digits, gx, peer = self.context
        d = self.order[self.phase]
        for copy in self.flying:
            copy.wait_recv()
        total = self.source[self.index(digits[d])]
        for k in range(1, sizes[d]):
            total = total + self.received[self.phase][k - 1]
        self.parts[self.phase][...] = total
        self.source = self.parts[self.phase]
        self.left.remove(d)
        self.phase += 1


def kernel(geometry, grid4, rows_in, pot_in, eig, corr_out, ham_out, rot_out, flat, pot, coef, padded, hq,
           corr, ham, halo_y, halo_x, pair_c, pair_h, sum_c, sum_h, gx_c, gx_h, final_c, final_h,
           send_sems, recv_sems, local_sems, *buffers):
    gx_size, gyz_size, cx, cy, cz, bands, rows, sizes, copy_count = geometry
    count = len(sizes)
    half = bands // 2
    gx, gyz = lax.axis_index("gx"), lax.axis_index("gyz")
    parity = lax.rem(gx, 2)
    partner = gx + 1 - 2 * parity
    mine = pl.ds(pl.multiple_of(parity * half, half), half)
    other = pl.ds(pl.multiple_of((1 - parity) * half, half), half)
    strides = []
    step = gyz_size
    for size in sizes:
        step //= size
        strides.append(step)
    digits = [lax.rem(gyz // stride, size) for stride, size in zip(strides, sizes)]
    copies = Copies(send_sems, recv_sems)

    def peer(d, k):
        digit = lax.rem(digits[d] + k, sizes[d])
        return gyz + (digit - digits[d]) * strides[d], digit

    load_flat = pltpu.make_async_copy(rows_in, flat, local_sems.at[0])
    load_flat.start()
    own_coef = coef.at[tuple(digits) + (slice(None), mine)]
    load_coef = pltpu.make_async_copy(eig.at[:, mine], own_coef, local_sems.at[1])
    load_coef.start()
    load_pot = pltpu.make_async_copy(pot_in, pot, local_sems.at[2])
    load_pot.start()

    barrier = pltpu.get_barrier_semaphore()
    greeted = [(gx, lax.rem(gyz + 1, gyz_size)), (gx, lax.rem(gyz + gyz_size - 1, gyz_size)),
               (lax.rem(gx + 1, gx_size), gyz), (lax.rem(gx + gx_size - 1, gx_size), gyz),
               (partner, gyz)]
    for d, size in enumerate(sizes):
        greeted += [(gx, peer(d, k)[0]) for k in range(1, size)]
    greeted += [(lax.rem(gx + 2 * k, gx_size), gyz) for k in range(1, gx_size // 2)]
    for device in greeted:
        pl.semaphore_signal(barrier, inc=1, device_id=device, device_id_type=MESH)
    pl.semaphore_wait(barrier, len(greeted))

    to_x = copies.make(grid4.at[cx - 1], halo_x, (lax.rem(gx + 1, gx_size), gyz))
    to_y = copies.make(grid4.at[:, cy - 1], halo_y, (gx, lax.rem(gyz + 1, gyz_size)))
    last_x, last_y = gx == gx_size - 1, gyz == gyz_size - 1

    @pl.when(jnp.logical_not(last_y))
    def _():
        to_y.start()

    @pl.when(jnp.logical_not(last_x))
    def _():
        to_x.start()

    @pl.when(gx == 0)
    def _():
        halo_x[...] = jnp.zeros_like(halo_x)

    @pl.when(gyz == 0)
    def _():
        halo_y[...] = jnp.zeros_like(halo_y)

    sent = []

    def coef_phase(d):
        started = []
        for k in range(1, sizes[d]):
            index = tuple([slice(None)] * d + digits[d:]) + (slice(None), mine)
            block = coef.at[index]
            copy = copies.make(block, block, (gx, peer(d, k)[0]))
            copy.start()
            started.append(copy)
        sent.extend(started)
        return started

    def block_index(block):
        index = []
        for stride in strides:
            index.append(block // stride)
            block %= stride
        return tuple(index)

    def store_rows(target, first, value):
        for j in range(value.shape[0] // rows):
            target[block_index(first // rows + j)] = value[j * rows:(j + 1) * rows]

    tile = min(bands, 256)
    load_flat.wait()
    for first in range(0, bands, tile):
        store_rows(corr, first, gram_t(flat[:, first:first + tile], flat[...]))
    everything = tuple([slice(None)] * (count + 1))
    pair_copy_c = copies.make(corr.at[everything + (other,)], pair_c, (partner, gyz))
    pair_copy_c.start()
    load_coef.wait()
    load_pot.wait()

    plane = cy * cz
    cells = cx * plane
    chunk = 2 * cz if cells % (2 * cz) == 0 else cz
    for first in range(0, cells, chunk):
        padded[first:first + chunk] = flat[first:first + chunk].astype(F32)
    row = lax.broadcasted_iota(jnp.int32, (cz, cz), 0)
    column = lax.broadcasted_iota(jnp.int32, (cz, cz), 1)
    zero_row = jnp.zeros((1, bands), F32)

    def segment(x, y):
        at = x * plane + y * cz
        centre = padded[at:at + cz]
        near = jnp.concatenate([zero_row, centre[:-1]]) + jnp.concatenate([centre[1:], zero_row])
        for there, offset in ((x > 0, -plane), (x < cx - 1, plane), (y > 0, -cz), (y < cy - 1, cz)):
            if there:
                near = near + padded[at + offset:at + offset + cz]
        local = jnp.broadcast_to(pot[y, x:x + 1, :], (cz, cz))
        factor = 3.0 + jnp.sum(jnp.where(row == column, local, 0.0), axis=1, keepdims=True)
        return factor * centre - 0.5 * near

    order = list(itertools.product(range(cx), range(cy)))
    per = chunk // cz
    for first in range(0, len(order), per):
        hq[first * cz:(first + per) * cz] = jnp.concatenate(
            [segment(*xy) for xy in order[first:first + per]]).astype(jnp.bfloat16)

    context = (copies, sizes, digits, gx, peer)
    ham_plan, corr_plan = streams_of(rows, count)
    taken = iter(buffers)

    def streams(plan, source):
        made = []
        for first, last, digit_order in plan:
            received = [next(taken) for _ in digit_order]
            parts = [next(taken) for _ in digit_order]
            made.append(Stream(context, source, first, last, digit_order, received, parts))
        return made

    ham_streams, corr_streams = streams(ham_plan, sum_h), streams(corr_plan, sum_c)

    def begin(group):
        for stream in group:
            stream.start()

    def end(group):
        for stream in group:
            stream.finish()
            sent.extend(stream.flying)
            if stream.phase < count:
                stream.start()

    pair_copy_c.wait_recv()
    sum_c[...] = corr[everything + (mine,)] + pair_c[...]
    begin(corr_streams)
    coef_copies = coef_phase(0)

    for first in range(0, bands, tile):
        store_rows(ham, first, gram_t(flat[:, first:first + tile], hq[...]))

    @pl.when(gyz > 0)
    def _():
        to_y.wait_recv()

    @pl.when(gx > 0)
    def _():
        to_x.wait_recv()

    first_y = jnp.concatenate([flat[x * plane:x * plane + cz] for x in range(cx)])
    ghost_y = jnp.concatenate([halo_y[x] for x in range(cx)])
    first_x = flat[0:plane]
    ghost_x = jnp.concatenate([halo_x[y] for y in range(cy)])
    cross = padded.at[0:bands]
    for first in range(0, bands, tile):
        cut = slice(first, first + tile)
        cross[cut] = -0.5 * (gram_t(first_y[:, cut], ghost_y) + gram_t(first_x[:, cut], ghost_x))
    for first in range(0, bands, tile):
        cut = slice(first, first + tile)
        value = cross[cut] + jnp.transpose(cross[:, cut])
        for j in range(tile // rows):
            index = block_index(first // rows + j)
            ham[index] = ham[index] + value[j * rows:(j + 1) * rows]
    pair_copy_h = copies.make(ham.at[everything + (other,)], pair_h, (partner, gyz))
    pair_copy_h.start()
    pair_copy_h.wait_recv()
    sum_h[...] = ham[everything + (mine,)] + pair_h[...]
    begin(ham_streams)

    for d in range(count):
        for copy in coef_copies:
            copy.wait_recv()
        coef_copies = coef_phase(d + 1) if d + 1 < count else []
    mine_block = coef.at[everything + (mine,)]
    pair_copy_e = copies.make(mine_block, mine_block, (partner, gyz))

    scale = 1.0 / (cells * gyz_size)

    def last_sum(group, gx_recv, final):
        for at, stream in enumerate(group):
            final[stream.rows, mine] = stream.source[...]
        others = []
        for k in range(1, gx_size // 2):
            target = (lax.rem(gx + 2 * k, gx_size), gyz)
            copy = copies.make(final.at[:, mine], gx_recv.at[k - 1], target)
            copy.start()
            others.append(copy)
        for copy in others:
            copy.wait()
        total = final[:, mine]
        for k in range(1, gx_size // 2):
            total = total + gx_recv[k - 1]
        final[:, mine] = total * scale
        copy = copies.make(final.at[:, mine], final.at[:, mine], (partner, gyz))
        copy.start()
        return copy

    end(corr_streams)
    pair_copy_e.start()
    end(ham_streams)
    pair_copy_e.wait_recv()
    whole = coef[...].reshape(bands, bands)
    part = max(size for size in range(16, 512, 16) if cells % size == 0)
    for first in range(0, cells, part):
        rot_out[first:first + part] = jnp.dot(
            flat[first:first + part], whole, preferred_element_type=F32).astype(jnp.bfloat16)

    for _ in range(count - 1):
        end(corr_streams)
    last_c = last_sum(corr_streams, gx_c, final_c)
    for _ in range(count - 1):
        end(ham_streams)
    last_h = last_sum(ham_streams, gx_h, final_h)

    last_c.wait_recv()
    corr_out[...] = final_c[...]
    last_h.wait_recv()
    ham_out[...] = final_h[...]
    for copy in sent + [pair_copy_c, pair_copy_h, pair_copy_e, last_c, last_h]:
        copy.wait_send()

    @pl.when(jnp.logical_not(last_y))
    def _():
        to_y.wait_send()

    @pl.when(jnp.logical_not(last_x))
    def _():
        to_x.wait_send()

    assert copies.used == copy_count


def deliver(corr, ham, rot, corr_out, ham_out, rot_out, sems):
    copies = [pltpu.make_async_copy(source, target, sems.at[i]) for i, (source, target) in
              enumerate(((rot, rot_out), (corr, corr_out), (ham, ham_out)))]
    for copy in copies:
        copy.start()
    for copy in copies:
        copy.wait()


def on_device(bands, potential, eigenvectors):
    gx_size, gyz_size = lax.axis_size("gx"), lax.axis_size("gyz")
    cx, cy, cz, width = bands.shape
    rows = eigenvectors.shape[0]
    cells = cx * cy * cz
    sizes = digit_sizes(gyz_size)
    count = len(sizes)
    half = width // 2
    flat = bands.reshape(cells, width)
    ham_plan, corr_plan = streams_of(rows, count)
    per_stream = sum(s - 1 for s in sizes)
    copy_count = 2 + (1 + len(ham_plan) + len(corr_plan)) * per_stream + 3 + 2 * (gx_size // 2)
    geometry = (gx_size, gyz_size, cx, cy, cz, width, rows, sizes, copy_count)

    buffers = []
    for first, last, order in ham_plan + corr_plan:
        received, parts, left = [], [], list(range(count))
        for d in order:
            left.remove(d)
            shape = tuple(sizes[i] for i in left) + (last - first, half)
            received.append(pltpu.VMEM((sizes[d] - 1,) + shape, F32))
            parts.append(pltpu.VMEM(shape, F32))
        buffers += received + parts

    wide, narrow = sizes + (rows, width), sizes + (rows, half)
    others = max(gx_size // 2 - 1, 1)
    vmem, anywhere = pl.BlockSpec(memory_space=pltpu.VMEM), pl.BlockSpec(memory_space=pl.ANY)
    results = (jax.ShapeDtypeStruct((rows, width), F32), jax.ShapeDtypeStruct((rows, width), F32),
               jax.ShapeDtypeStruct((cells, width), jnp.bfloat16))
    computed = pl.pallas_call(
        functools.partial(kernel, geometry),
        out_shape=results,
        in_specs=[pl.BlockSpec(memory_space=pltpu.HBM)] * 4,
        out_specs=(vmem, vmem, vmem),
        scratch_shapes=[
            pltpu.VMEM((cells, width), jnp.bfloat16), pltpu.VMEM((cy, cx, cz), F32),
            pltpu.VMEM(wide, jnp.bfloat16),
            pltpu.VMEM((cells, width), F32), pltpu.VMEM((cells, width), jnp.bfloat16),
            pltpu.VMEM(wide, F32), pltpu.VMEM(wide, F32),
            pltpu.VMEM((cx, cz, width), jnp.bfloat16), pltpu.VMEM((cy, cz, width), jnp.bfloat16),
            pltpu.VMEM(narrow, F32), pltpu.VMEM(narrow, F32),
            pltpu.VMEM(narrow, F32), pltpu.VMEM(narrow, F32),
            pltpu.VMEM((others, rows, half), F32), pltpu.VMEM((others, rows, half), F32),
            pltpu.VMEM((rows, width), F32), pltpu.VMEM((rows, width), F32),
            pltpu.SemaphoreType.DMA((copy_count,)), pltpu.SemaphoreType.DMA((copy_count,)),
            pltpu.SemaphoreType.DMA((3,)), *buffers,
        ],
        compiler_params=pltpu.CompilerParams(
            collective_id=0, has_side_effects=True, vmem_limit_bytes=52 * 1024 * 1024),
    )(bands, flat, jnp.transpose(potential, (1, 0, 2)), eigenvectors)
    corr, ham, rotated = pl.pallas_call(
        deliver, out_shape=results, in_specs=[vmem] * 3, out_specs=[anywhere] * 3,
        scratch_shapes=[pltpu.SemaphoreType.DMA((3,))],
        compiler_params=pltpu.CompilerParams(vmem_limit_bytes=8 * 1024 * 1024),
    )(*computed)
    return corr, ham, rotated.reshape(bands.shape)


def solution(mesh):
    in_specs = (P("gx", "gyz", None, None), P("gx", "gyz", None), P("gyz", None))
    out_specs = (P("gyz", None), P("gyz", None), P("gx", "gyz", None, None))
    return jax.shard_map(
        on_device, mesh=mesh, in_specs=in_specs, out_specs=out_specs, check_vma=False
    )
```

time: 46.8 us -> 37.1 us (0.79)
  Pallas kernels: 41 us -> 34.8 us
  matrix products: 2.18 us -> 0 us
  local copies, waits for them, and re-layouts: 2.75 us -> 1.48 us
    pallas_call x1 -> x2, Pallas kernels: 41 us -> 34.8 us  [the longest x1 33.5 us: on_device(): pl.pallas_call(functools.partial(kernel, geometry), out_shape=results, in...]
    dot_general x1 -> x0, matrix products: 2.18 us -> none  [on_device(): jnp.dot(flat, coef.reshape(width, width), preferred_element_type=F32)]
    unnamed x7 -> x4, local copies, waits for them, and re-layouts: 2.75 us -> 1.48 us
where the time goes in v2:
time: 37.1 us; the launch traced here: 36.9 us
  Pallas kernels  34.8 us (94%)
  local copies, waits for them, and re-layouts  1.48 us (4%)
  between operations  0.65 us (2%)
    pallas_call x1, Pallas kernels, on_device(): pl.pallas_call(functools.partial(kernel, geometry), out_shape=results, in...  33.5 us
    unnamed x4, local copies, waits for them, and re-layouts  1.48 us
    pallas_call x1, Pallas kernels, on_device(): pl.pallas_call(deliver, out_shape=results, in_specs=[vmem] * 3, out_specs...  1.22 us

profile of v2, /device:TPU:0, one launch (start us, length us, event | category | flops | bytes accessed | tf_op | source)
XLA Modules:
  0.0 36.9 jit_solution(14697017911200918193)
XLA Ops:
  0.6 0.0 copy-start
  0.6 0.7 %copy-done = bf16[32,512]{1,0:T(8,128)(2,1)S(1)} copy-done((bf16[32,512]{1,0:T(8,128)(2,1)S(1)}, bf16[32,512]{1,0:T(8,128)(2,1)}, u32[]{:S(2)}) %copy-start) | copy-done | bytes 32792
  1.4 0.0 copy-start.1
  1.4 0.7 %copy-done.1 = f32[8,5,40]{2,0,1:T(8,128)S(1)} copy-done((f32[8,5,40]{2,0,1:T(8,128)S(1)}, f32[8,5,40]{2,0,1:T(8,128)}, u32[]{:S(2)}) %copy-start.1) | copy-done | bytes 6424
  2.1 33.5 %shard_map.58 = (f32[32,512]{1,0:T(8,128)S(1)}, f32[32,512]{1,0:T(8,128)S(1)}, bf16[1600,512]{1,0:T(8,128)(2,1)S(1)}) custom-call(bf16[8,5,40,512]{3,2,1,0:T(8,128)(2,1)} %grid4.1, bf16[1600,512]{1,0:T(8,128)(2,1)} %bitcast.4, f32[5,8,40]{2,1,0:T(8,128)S(1)} %bitcast.3, bf16[32,512]{1,0:T(8,128)(2,1)S(1)} %copy-done), custom_call_target="tpu_custom_call" | custom-call | tf_op jit(solution)/shard_map/pallas_call | solution.py:371
  35.7 1.2 %shard_map.59 = (f32[32,512]{1,0:T(8,128)}, f32[32,512]{1,0:T(8,128)}, bf16[1600,512]{1,0:T(8,128)(2,1)}) custom-call(f32[32,512]{1,0:T(8,128)S(1)} %get-tuple-element.9.corr, f32[32,512]{1,0:T(8,128)S(1)} %get-tuple-element.10.ham, bf16[1600,512]{1,0:T(8,128)(2,1)S(1)} %get-tuple-element.11.rot), custom_call_target="tpu_custom_call" | custom-call | tf_op jit(solution)/shard_map/pallas_call | solution.py:392
Async XLA Ops:
  0.6 0.8 %copy-start = (bf16[32,512]{1,0:T(8,128)(2,1)S(1)}, bf16[32,512]{1,0:T(8,128)(2,1)}, u32[]{:S(2)}) copy-start(bf16[32,512]{1,0:T(8,128)(2,1)} %eig.1) | copy-start | bytes 98308
  1.4 0.7 %copy-start.1 = (f32[8,5,40]{2,0,1:T(8,128)S(1)}, f32[8,5,40]{2,0,1:T(8,128)}, u32[]{:S(2)}) copy-start(f32[8,5,40]{2,0,1:T(8,128)} %param.4) | copy-start | bytes 19204

commit v3 on v2

--- a/solution.py
+++ b/solution.py
@@ -39,13 +39,16 @@
 
 def streams_of(rows, count):
     fast, slow = tuple(range(count))[::-1], tuple(range(count))
-    if rows % 32 == 0 and count > 1:
-        cut = rows // 4
-        return ((0, cut * H_PARTS, fast), (cut * H_PARTS, rows, slow)), ((0, cut * C_PARTS, fast), (cut * C_PARTS, rows, slow))
-    return ((0, rows, fast),), ((0, rows, fast),)
-
-
-H_PARTS, C_PARTS = 3, 2
+    if rows % 32 or count == 1:
+        return ((0, rows, fast),), ((0, rows, fast),)
+    plans = []
+    for parts in (H_PARTS, C_PARTS):
+        cut = rows // 4 * parts
+        plans.append(tuple(p for p in ((0, cut, fast), (cut, rows, slow)) if p[1] > p[0]))
+    return tuple(plans)
+
+
+H_PARTS, C_PARTS = 4, 2
 
 
 class Stream:
@@ -85,7 +88,7 @@
 
 
 def kernel(geometry, grid4, rows_in, pot_in, eig, corr_out, ham_out, rot_out, flat, pot, coef, padded, hq,
-           corr, ham, halo_y, halo_x, pair_c, pair_h, sum_c, sum_h, gx_c, gx_h, final_c, final_h,
+           corr, ham, halo_y, halo_x, pair_c, pair_h, sum_c, sum_h, gx_c, gx_h,
            send_sems, recv_sems, local_sems, *buffers):
     gx_size, gyz_size, cx, cy, cz, bands, rows, sizes, copy_count = geometry
     count = len(sizes)
@@ -126,38 +129,46 @@
         pl.semaphore_signal(barrier, inc=1, device_id=device, device_id_type=MESH)
     pl.semaphore_wait(barrier, len(greeted))
 
-    to_x = copies.make(grid4.at[cx - 1], halo_x, (lax.rem(gx + 1, gx_size), gyz))
-    to_y = copies.make(grid4.at[:, cy - 1], halo_y, (gx, lax.rem(gyz + 1, gyz_size)))
-    last_x, last_y = gx == gx_size - 1, gyz == gyz_size - 1
-
-    @pl.when(jnp.logical_not(last_y))
-    def _():
-        to_y.start()
-
-    @pl.when(jnp.logical_not(last_x))
-    def _():
-        to_x.start()
-
-    @pl.when(gx == 0)
-    def _():
-        halo_x[...] = jnp.zeros_like(halo_x)
-
-    @pl.when(gyz == 0)
-    def _():
-        halo_y[...] = jnp.zeros_like(halo_y)
-
     sent = []
 
     def coef_phase(d):
         started = []
         for k in range(1, sizes[d]):
-            index = tuple([slice(None)] * d + digits[d:]) + (slice(None), mine)
+            index = tuple(digits[:d + 1] + [slice(None)] * (count - 1 - d)) + (slice(None), mine)
             block = coef.at[index]
             copy = copies.make(block, block, (gx, peer(d, k)[0]))
             copy.start()
             started.append(copy)
         sent.extend(started)
         return started
+
+    def next_coef_phase(started, d):
+        for copy in started:
+            copy.wait_recv()
+        return coef_phase(count - 1 - d) if d < count else []
+
+    load_coef.wait()
+    coef_copies = coef_phase(count - 1)
+
+    to_x = copies.make(grid4.at[cx - 1], halo_x, (lax.rem(gx + 1, gx_size), gyz))
+    to_y = copies.make(grid4.at[:, cy - 1], halo_y, (gx, lax.rem(gyz + 1, gyz_size)))
+    last_x, last_y = gx == gx_size - 1, gyz == gyz_size - 1
+
+    @pl.when(jnp.logical_not(last_y))
+    def _():
+        to_y.start()
+
+    @pl.when(jnp.logical_not(last_x))
+    def _():
+        to_x.start()
+
+    @pl.when(gx == 0)
+    def _():
+        halo_x[...] = jnp.zeros_like(halo_x)
+
+    @pl.when(gyz == 0)
+    def _():
+        halo_y[...] = jnp.zeros_like(halo_y)
 
     def block_index(block):
         index = []
@@ -177,7 +188,6 @@
     everything = tuple([slice(None)] * (count + 1))
     pair_copy_c = copies.make(corr.at[everything + (other,)], pair_c, (partner, gyz))
     pair_copy_c.start()
-    load_coef.wait()
     load_pot.wait()
 
     plane = cy * cz
@@ -234,7 +244,7 @@
     pair_copy_c.wait_recv()
     sum_c[...] = corr[everything + (mine,)] + pair_c[...]
     begin(corr_streams)
-    coef_copies = coef_phase(0)
+    coef_copies = next_coef_phase(coef_copies, 1)
 
     for first in range(0, bands, tile):
         store_rows(ham, first, gram_t(flat[:, first:first + tile], hq[...]))
@@ -267,12 +277,11 @@
     sum_h[...] = ham[everything + (mine,)] + pair_h[...]
     begin(ham_streams)
 
-    for d in range(count):
-        for copy in coef_copies:
-            copy.wait_recv()
-        coef_copies = coef_phase(d + 1) if d + 1 < count else []
+    for d in range(2, count + 1):
+        coef_copies = next_coef_phase(coef_copies, d)
     mine_block = coef.at[everything + (mine,)]
     pair_copy_e = copies.make(mine_block, mine_block, (partner, gyz))
+    pair_copy_e.start()
 
     scale = 1.0 / (cells * gyz_size)
 
@@ -296,7 +305,6 @@
         return copy
 
     end(corr_streams)
-    pair_copy_e.start()
     end(ham_streams)
     pair_copy_e.wait_recv()
     whole = coef[...].reshape(bands, bands)
@@ -307,15 +315,13 @@
 
     for _ in range(count - 1):
         end(corr_streams)
-    last_c = last_sum(corr_streams, gx_c, final_c)
+    last_c = last_sum(corr_streams, gx_c, corr_out)
     for _ in range(count - 1):
         end(ham_streams)
-    last_h = last_sum(ham_streams, gx_h, final_h)
+    last_h = last_sum(ham_streams, gx_h, ham_out)
 
     last_c.wait_recv()
-    corr_out[...] = final_c[...]
     last_h.wait_recv()
-    ham_out[...] = final_h[...]
     for copy in sent + [pair_copy_c, pair_copy_h, pair_copy_e, last_c, last_h]:
         copy.wait_send()
 
@@ -337,6 +343,10 @@
         copy.start()
     for copy in copies:
         copy.wait()
+
+
+def in_hbm(array):
+    return pltpu.with_memory_space_constraint(array, pltpu.HBM)
 
 
 def on_device(bands, potential, eigenvectors):
@@ -382,13 +392,12 @@
             pltpu.VMEM(narrow, F32), pltpu.VMEM(narrow, F32),
             pltpu.VMEM(narrow, F32), pltpu.VMEM(narrow, F32),
             pltpu.VMEM((others, rows, half), F32), pltpu.VMEM((others, rows, half), F32),
-            pltpu.VMEM((rows, width), F32), pltpu.VMEM((rows, width), F32),
             pltpu.SemaphoreType.DMA((copy_count,)), pltpu.SemaphoreType.DMA((copy_count,)),
             pltpu.SemaphoreType.DMA((3,)), *buffers,
         ],
         compiler_params=pltpu.CompilerParams(
             collective_id=0, has_side_effects=True, vmem_limit_bytes=52 * 1024 * 1024),
-    )(bands, flat, jnp.transpose(potential, (1, 0, 2)), eigenvectors)
+    )(bands, flat, in_hbm(jnp.transpose(potential, (1, 0, 2))), in_hbm(eigenvectors))
     corr, ham, rotated = pl.pallas_call(
         deliver, out_shape=results, in_specs=[vmem] * 3, out_specs=[anywhere] * 3,
         scratch_shapes=[pltpu.SemaphoreType.DMA((3,))],

time: 37.1 us -> 33.1 us (0.89)
  Pallas kernels: 34.8 us -> 32 us
  local copies, waits for them, and re-layouts: 1.48 us -> 0 us
    pallas_call x1, Pallas kernels: 33.5 us -> 30.8 us  [on_device(): pl.pallas_call(functools.partial(kernel, geometry), out_shape=results, in...]
    unnamed x4 -> x0, local copies, waits for them, and re-layouts: 1.48 us -> none
where the time goes in v3:
time: 33.1 us; the launch traced here: 32.6 us
  Pallas kernels  32 us (97%)
  between operations  0.64 us (2%)
    pallas_call x1, Pallas kernels, on_device(): pl.pallas_call(functools.partial(kernel, geometry), out_shape=results, in...  30.8 us
    pallas_call x1, Pallas kernels, on_device(): pl.pallas_call(deliver, out_shape=results, in_specs=[vmem] * 3, out_specs...  1.22 us

profile of v3, /device:TPU:0, one launch (start us, length us, event | category | flops | bytes accessed | tf_op | source)
XLA Modules:
  0.0 32.6 jit_solution(16364790490611537705)
XLA Ops:
  0.6 30.8 %shard_map.58 = (f32[32,512]{1,0:T(8,128)S(1)}, f32[32,512]{1,0:T(8,128)S(1)}, bf16[1600,512]{1,0:T(8,128)(2,1)S(1)}) custom-call(bf16[8,5,40,512]{3,2,1,0:T(8,128)(2,1)} %grid4.1, bf16[1600,512]{1,0:T(8,128)(2,1)} %bitcast.3, f32[5,8,40]{2,1,0:T(8,128)} %bitcast.4, bf16[32,512]{1,0:T(8,128)(2,1)} %eig.1), custom_call_target="tpu_custom_call" | custom-call | tf_op jit(solution)/shard_map/pallas_call | solution.py:381
  31.4 1.2 %shard_map.59 = (f32[32,512]{1,0:T(8,128)}, f32[32,512]{1,0:T(8,128)}, bf16[1600,512]{1,0:T(8,128)(2,1)}) custom-call(f32[32,512]{1,0:T(8,128)S(1)} %get-tuple-element.9.corr, f32[32,512]{1,0:T(8,128)S(1)} %get-tuple-element.10.ham, bf16[1600,512]{1,0:T(8,128)(2,1)S(1)} %get-tuple-element.11.rot), custom_call_target="tpu_custom_call" | custom-call | tf_op jit(solution)/shard_map/pallas_call | solution.py:401
